TPU v7x, 32 devices: a whole 2x2x4 slice. The times are simulated.
32 devices in a mesh: layer: 8 (over y, x, core), tensor: 4 (over z).
Axes of the slice: x: 2, y: 2, z: 4, core: 2. Of those that a mesh axis runs over, the one named last changes fastest.
Arguments:
- gradient: bfloat16 [8, 1024, 8192], P(None, 'tensor', 'layer'), may hold values from -8 to 8
- row_basis: bfloat16 [8, 1024, 256], P('layer', 'tensor'), may hold values from -0.1875 to 0.1875
- column_basis: bfloat16 [8, 8192, 256], P('layer', 'tensor'), may hold values from -0.0625 to 0.0625
- row_eigen: float32 [8, 256], P('layer'), may hold values from 0.01 to 10
- column_eigen: float32 [8, 256], P('layer'), may hold values from 0.01 to 10
- row_escape: float32 [8], P('layer'), may hold values from 0.02 to 0.2
- column_escape: float32 [8], P('layer'), may hold values from 0.02 to 0.2
Outputs:
- update: bfloat16 [8, 1024, 8192], P(None, 'tensor', 'layer')
All inputs are finite; a program needn't handle non-finite values.
Results may differ from a plain program's by a relative error of at most 0.0055.
Values may be sent and summed in bfloat16 or wider, within the bound.
A program may use at most 128 MiB of HBM per device.

v0:
```python
import jax
import jax.numpy as jnp
from jax import lax
from jax.sharding import PartitionSpec as P


def coefficients(row_eigen, column_eigen, row_escape, column_escape):
    row_base = row_escape ** (-0.25)
    column_base = column_escape ** (-0.25)
    row_coef = (row_eigen + row_escape[:, None]) ** (-0.25) - row_base[:, None]
    column_coef = (column_eigen + column_escape[:, None]) ** (-0.25) - column_base[:, None]
    return (row_base, column_base, row_coef, column_coef)


def group_norm(local_block):
    partial_sq = jnp.sum(jnp.square(local_block.astype(jnp.float32)), axis=(1, 2))
    return lax.psum(partial_sq, "tensor")


def finish(raw_update, grad_sq):
    update_sq = lax.psum(jnp.sum(jnp.square(raw_update), axis=(1, 2)), "tensor")
    factor = jnp.sqrt((grad_sq + 1.0) / (update_sq + 1.0))
    return (raw_update * factor[:, None, None]).astype(jnp.bfloat16)


def body(gradient, row_basis, column_basis, row_eigen, column_eigen, row_escape, column_escape):
    row_base, column_base, row_coef, column_coef = coefficients(
        row_eigen, column_eigen, row_escape, column_escape
    )
    both_base = (row_base * column_base)[:, None, None]
    group_block = lax.all_to_all(gradient, "layer", split_axis=0, concat_axis=2, tiled=True)
    grad_sq = group_norm(group_block)
    own_proj = lax.psum_scatter(
        jnp.einsum(
            "lrk,lrd->dlk", row_basis, group_block, preferred_element_type=jnp.float32
        ).astype(jnp.bfloat16),
        "tensor",
        scatter_dimension=0,
        tiled=True,
    ).astype(jnp.float32)
    scaled = (own_proj * row_coef[None]).astype(jnp.bfloat16)
    core_part = jnp.einsum("dlk,ldj->lkj", scaled, column_basis, preferred_element_type=jnp.float32)
    core_mat = lax.psum(core_part.astype(jnp.bfloat16), "tensor")
    whole_columns = lax.all_gather(column_basis, "tensor", axis=1, tiled=True)
    middle = jnp.einsum(
        "lrd,ldk->lrk", group_block, whole_columns, preferred_element_type=jnp.float32
    )
    row_term = jnp.einsum(
        "lrk,dlk->lrd",
        row_basis,
        lax.all_gather(scaled, "tensor", axis=0, tiled=True),
        preferred_element_type=jnp.float32,
    )
    mixed = row_base[:, None, None] * middle + jnp.einsum(
        "lrk,lkj->lrj", row_basis, core_mat, preferred_element_type=jnp.float32
    )
    left_factor = (mixed * column_coef[:, None, :]).astype(jnp.bfloat16)
    raw_update = both_base * group_block.astype(jnp.float32) + column_base[:, None, None] * row_term
    raw_update = raw_update + jnp.einsum(
        "lrk,ldk->lrd", left_factor, whole_columns, preferred_element_type=jnp.float32
    )
    rows_block = finish(raw_update, grad_sq)
    return lax.all_to_all(rows_block, "layer", split_axis=2, concat_axis=0, tiled=True)


def solution(mesh):
    in_specs = (
        P(None, "tensor", "layer"),
        P("layer", "tensor", None),
        P("layer", "tensor", None),
        P("layer", None),
        P("layer", None),
        P("layer"),
        P("layer"),
    )
    out_specs = P(None, "tensor", "layer")
    return jax.shard_map(body, mesh=mesh, in_specs=in_specs, out_specs=out_specs, check_vma=False)
```

profile of v0, /device:TPU:0, one launch (start us, length us, event | category | flops | bytes accessed | tf_op | source)
XLA Modules:
  0.0 558.4 jit_solution(9425964493506922182)
XLA Ops:
  6.5 0.0 copy-start
  6.5 0.0 reduce-scatter.2.cloned.1.call-start
  6.5 54.5 %all_to_all.36 = bf16[8,256,1024]{2,1,0:T(8,128)(2,1)} all-to-all(bf16[8,256,1024]{2,1,0:T(8,128)(2,1)} %param.7), channel_id=1, replica_groups=mesh['layer'=8,'tensor'=4] {'layer'}, dimensions={0} | all-to-all | bytes 8388608 | tf_op jit(solution)/shard_map/all_to_all | solution.py:31
  61.0 6.4 %copy.15 = bf16[1,256,8,1024]{1,3,2,0:T(8,128)(2,1)} copy(bf16[1,256,8,1024]{3,1,2,0:T(8,128)(2,1)} %bitcast.80) | data formatting | bytes 8388608 | tf_op jit(solution)/shard_map/all_to_all | solution.py:31
  67.4 0.0 copy-done
  67.4 5.4 fusion.2
  72.8 0.0 copy-start.4
  72.8 0.0 copy-start.5
  72.8 0.0 reduce-scatter.2.cloned.1.call-update
  72.9 0.0 all-gather.5.cloned.1.call-start
  72.9 0.7 all-gather.5.cloned.1.call-update
  73.6 0.0 all-gather.3.cloned.1.call-start
  74.4 0.0 copy-done.4
  74.4 75.4 %reduce-scatter.2.cloned.1.call-done = bf16[2048,1,256]{2,0,1:T(8,128)(2,1)} async-done(((bf16[8192,1,256]{2,0,1:T(8,128)(2,1)}), bf16[2048,1,256]{2,0,1:T(8,128)(2,1)}) %reduce-scatter.2.cloned.1.call-update) | async-done | bytes 1048592 | tf_op jit(solution)/shard_map/reduce_scatter | solution.py:33
  149.8 2.4 multiply_convert_fusion.1
  152.2 0.0 all-gather.3.cloned.1.call-update
  152.3 0.0 all-reduce.3.cloned.1.call-start
  153.0 0.0 copy-done.5
  153.0 4.9 multiply_reduce_fusion.1
  157.9 0.0 copy-start.2
  158.0 0.0 copy-start.3
  158.0 74.7 %all-gather.5.cloned.1.call-done = bf16[1,8192,256]{2,1,0:T(8,128)(2,1)} async-done(((bf16[1,2048,256]{2,1,0:T(8,128)(2,1)}), bf16[1,8192,256]{2,1,0:T(8,128)(2,1)}) %all-gather.5.cloned.1.call-update) | async-done | bytes 4194320 | tf_op jit(solution)/shard_map/all_gather | solution.py:44
  232.7 4.8 fusion.10
  237.4 0.0 copy-done.2
  237.4 0.0 copy-done.3
  237.5 1.1 convolution_convert_fusion.1
  238.6 0.0 all-reduce.3.cloned.1.call-update
  238.6 75.0 %all-gather.3.cloned.1.call-done = bf16[8192,1,256]{2,0,1:T(8,128)(2,1)} async-done(((bf16[2048,1,256]{2,0,1:T(8,128)(2,1)}), bf16[8192,1,256]{2,0,1:T(8,128)(2,1)}) %all-gather.3.cloned.1.call-update) | async-done | bytes 4194320 | tf_op jit(solution)/shard_map/all_gather | solution.py:51
  313.6 8.0 %fusion.1 = f32[256,8192]{0,1:T(8,128)} fusion(bf16[256,8192]{0,1:T(8,128)(2,1)} %bitcast.79, bf16[8192,1,256]{2,0,1:T(8,128)(2,1)} %all-gather.3.cloned.1.call-done, f32[]{:T(128)} %bitcast.4, f32[]{:T(128)} %bitcast, bf16[1,256,256]{2,1,0:T(8,128)(2,1)S(1)} %copy-done), kind=kOutput, calls=%fused_computation.3 | convolution fusion | flops 1082130432 | bytes 16908296 | tf_op jit(solution)/shard_map/lrk,dlk->lrd/dot_general | solution.py:48
  321.6 27.3 %all-reduce.3.cloned.1.call-done = bf16[256,256]{1,0:T(8,128)(2,1)} async-done(((bf16[256,256]{1,0:T(8,128)(2,1)}), bf16[256,256]{1,0:T(8,128)(2,1)}) %all-reduce.3.cloned.1.call-update) | async-done | bytes 131088 | tf_op jit(solution)/shard_map/psum | solution.py:43
  348.9 11.0 %multiply_reduce_fusion = (f32[]{:T(128)}, f32[256,8192]{0,1:T(8,128)}) fusion(f32[256,8192]{0,1:T(8,128)} %fusion.1, bf16[1,8192,256]{2,1,0:T(8,128)(2,1)} %all-gather.5.cloned.1.call-done, f32[256,256]{1,0:T(8,128)S(1)} %fusion.10, bf16[256,256]{1,0:T(8,128)(2,1)} %all-reduce.3.cloned.1.call-done, bf16[1,256,256]{2,1,0:T(8,128)(2,1)S(1)} %copy-done, ...), kind=kOutput, calls=%fused_computation.7 | convolution fusion | flops 1113784320 | bytes 21496836 | tf_op jit(solution)/shard_map/lrk,ldk->lrd/dot_general | solution.py:59
  359.9 11.3 %all-reduce = (f32[1]{0:T(128)}, f32[1]{0:T(128)}) all-reduce(f32[1]{0:T(128)} %bitcast.19, f32[1]{0:T(128)} %bitcast.20), channel_id=1, replica_groups=mesh['layer'=8,'tensor'=4] {'tensor'}, use_global_device_ids=true, to_apply=%region_3.0 | all-reduce | flops 2 | bytes 16 | tf_op jit(solution)/shard_map/psum | solution.py:17
  372.5 4.1 fusion.3
  376.5 49.5 %copy.24 = bf16[1,256,8192]{1,0,2:T(2,128)(2,1)} copy(bf16[1,256,8192]{1,2,0:T(8,128)(2,1)S(1)} %fusion.3) | data formatting | bytes 8388608 | tf_op jit(solution)/shard_map/convert_element_type | solution.py:23
  426.1 0.5 broadcast.23
  426.6 43.5 %reduce.4 = bf16[8192,256]{1,0:T(8,128)(2,1)} reduce(bf16[8192,1,256]{2,1,0:T(2,128)(2,1)} %bitcast.81, bf16[]{:T(256)} %broadcast.23), dimensions={1}, to_apply=%bitcast.74.reduce_sub_computation | reduce | bytes 8388610
  470.1 7.0 %reshape.90 = bf16[8,2,131072]{2,1,0:T(2,128)(2,1)} reshape(bf16[8192,256]{1,0:T(8,128)(2,1)} %reduce.4) | data formatting | bytes 8388608
  477.1 53.6 %all_to_all.37 = bf16[8,2,131072]{2,1,0:T(2,128)(2,1)} all-to-all(bf16[8,2,131072]{2,1,0:T(2,128)(2,1)} %reshape.90), channel_id=1, replica_groups=mesh['layer'=8,'tensor'=4] {'layer'}, dimensions={0} | all-to-all | bytes 8388608 | tf_op jit(solution)/shard_map/all_to_all | solution.py:63
  530.6 8.7 %reshape.91 = bf16[8192,1,256]{2,1,0:T(2,128)(2,1)} reshape(bf16[8,2,131072]{2,1,0:T(2,128)(2,1)} %all_to_all.37) | data formatting | bytes 8388608
  539.4 6.1 %copy.22 = bf16[1,256,8192]{1,2,0:T(8,128)(2,1)} copy(bf16[1,256,8192]{1,0,2:T(2,128)(2,1)} %bitcast.82) | data formatting | bytes 8388608
  545.4 0.0 copy-start.1
  545.4 6.5 %copy.19 = bf16[8,256,1024]{2,1,0:T(8,128)(2,1)} copy(bf16[8,256,1024]{1,2,0:T(8,128)(2,1)} %bitcast.83) | data formatting | bytes 8388608 | tf_op jit(solution)/shard_map/all_to_all | solution.py:63
  551.9 0.0 copy-done.1
  (2 shorter events, 0.0 us)
Async XLA Ops:
  6.5 60.9 %copy-start = (bf16[1,256,256]{2,1,0:T(8,128)(2,1)S(1)}, bf16[1,256,256]{2,1,0:T(8,128)(2,1)}, u32[]{:S(2)}) copy-start(bf16[1,256,256]{2,1,0:T(8,128)(2,1)} %param.8) | copy-start | bytes 393220
  6.5 143.3 %reduce-scatter.2.cloned.1.call-start = ((), (), s32[]{:S(2)}) async-start(), calls=%async_computation.3 | async-start | bytes 5242880 | tf_op jit(solution)/shard_map/reduce_scatter | solution.py:33
  72.8 1.5 copy-start.4
  72.8 80.2 %copy-start.5 = (f32[1,256]{1,0:T(1,128)S(1)}, f32[1,256]{1,0:T(1,128)}, u32[]{:S(2)}) copy-start(f32[1,256]{1,0:T(1,128)} %param.11) | copy-start | bytes 3076
  72.9 159.8 %all-gather.5.cloned.1.call-start = ((), (), s32[]{:S(2)}) async-start(), calls=%async_computation.5 | async-start | bytes 5242880 | tf_op jit(solution)/shard_map/all_gather | solution.py:44
  73.6 239.9 %all-gather.3.cloned.1.call-start = ((), (), s32[]{:S(2)}) async-start(), calls=%async_computation.4 | async-start | bytes 5242880 | tf_op jit(solution)/shard_map/all_gather | solution.py:51
  152.3 196.6 %all-reduce.3.cloned.1.call-start = ((), (), s32[]{:S(2)}) async-start(), calls=%async_computation.6 | async-start | bytes 262144 | tf_op jit(solution)/shard_map/psum | solution.py:43
  157.9 79.5 %copy-start.2 = (bf16[2048,1,256]{2,0,1:T(8,128)(2,1)S(1)}, bf16[2048,1,256]{2,0,1:T(8,128)(2,1)}, u32[]{:S(2)}) copy-start(bf16[2048,1,256]{2,0,1:T(8,128)(2,1)} %multiply_convert_fusion.1) | copy-start | bytes 3145732
  158.0 79.5 %copy-start.3 = (bf16[1,2048,256]{2,1,0:T(8,128)(2,1)S(1)}, bf16[1,2048,256]{2,1,0:T(8,128)(2,1)}, u32[]{:S(2)}) copy-start(bf16[1,2048,256]{2,1,0:T(8,128)(2,1)} %param.9) | copy-start | bytes 3145732
  545.4 6.5 %copy-start.1 = (bf16[1,256,256]{2,1,0:T(8,128)(2,1)S(1)}, bf16[1,256,256]{2,1,0:T(8,128)(2,1)}, u32[]{:S(2)}) copy-start(bf16[1,256,256]{2,1,0:T(8,128)(2,1)} %param.8) | copy-start | bytes 393220
Sparse Core Ops, SparseCore 0:
  73.0 76.7 reduce-scatter.1
  151.4 81.2 all-gather.4
  234.3 79.2 all-gather.2
  315.7 33.1 all-reduce.2
where the time goes:
time: 559 us; the launch traced here: 558 us
  waiting for transfers between devices  253 us (45%)
  blocking collectives  119 us (21%)
  local copies, waits for them, and re-layouts  84.7 us (15%)
  other arithmetic  54.9 us (10%)
  matrix products  30.3 us (5%)
  between operations  15.9 us (3%)
    reduce_scatter x1, waiting for transfers between devices, body(): lax.psum_scatter(jnp.einsum('lrk,lrd->dlk', row_basis, group_block, prefe...  75.4 us
    all_gather x1, waiting for transfers between devices, body(): lax.all_gather(scaled, 'tensor', axis=0, tiled=True)  75 us
    all_gather x1, waiting for transfers between devices, body(): whole_columns = lax.all_gather(column_basis, 'tensor', axis=1, tiled=True)  74.7 us
    all_to_all x1, blocking collectives, body(): lax.all_to_all(gradient, 'layer', split_axis=0, concat_axis=2, tiled=True)  54.5 us
    all_to_all x1, blocking collectives, body(): lax.all_to_all(rows_block, 'layer', split_axis=2, concat_axis=0, tiled=True)  53.6 us
    convert_element_type x1, local copies, waits for them, and re-layouts, finish(): return (raw_update * factor[:, None, None]).astype(jnp.bfloat16)  49.5 us
    unnamed x1, other arithmetic  43.5 us
    psum x1, waiting for transfers between devices, body(): core_mat = lax.psum(core_part.astype(jnp.bfloat16), 'tensor')  27.3 us
  transfers between devices with their start and end apart: 4, of which 4 were waited for; matrix products, arithmetic and copies ran while one was open for 4% of the time, Pallas kernels for 0%

commit v1 on v0

--- a/solution.py
+++ b/solution.py
@@ -2,6 +2,27 @@
 import jax.numpy as jnp
 from jax import lax
 from jax.sharding import PartitionSpec as P
+
+
+def _pass_flows(packet, axis_no):
+    packet = jnp.moveaxis(packet, 0, axis_no)
+    next_value = packet.shape
+    return packet.reshape(
+        *next_value[:axis_no],
+        next_value[axis_no] * next_value[axis_no + 1],
+        *next_value[axis_no + 2 :]
+    )
+
+
+def supply_the_point(frame, net_axis, row_dim):
+    amount_of = lax.axis_size(net_axis)
+    trail = tuple(((t, (t + 1) % amount_of) for t in range(amount_of)))
+    views = [frame]
+    while len(views) < amount_of:
+        views.append(lax.ppermute(views[-1], net_axis, trail))
+    even = lax.axis_index(net_axis)
+    views = jnp.stack(views, 0)[(even - jnp.arange(amount_of)) % amount_of]
+    return _pass_flows(views, row_dim)
 
 
 def coefficients(row_eigen, column_eigen, row_escape, column_escape):
@@ -48,7 +69,7 @@
     row_term = jnp.einsum(
         "lrk,dlk->lrd",
         row_basis,
-        lax.all_gather(scaled, "tensor", axis=0, tiled=True),
+        supply_the_point(scaled, "tensor", 0),
         preferred_element_type=jnp.float32,
     )
     mixed = row_base[:, None, None] * middle + jnp.einsum(

time: 559 us -> 522 us (0.934)
  waiting for transfers between devices: 253 us -> 175 us
  starting transfers between devices: 0.12 us -> 32.8 us
    ppermute x0 -> x3, waiting for transfers between devices: none -> 96.5 us  [supply_the_point(): views.append(lax.ppermute(views[-1], net_axis, trail))]
    all_gather x1 -> x0, waiting for transfers between devices: 75 us -> none  [body(): lax.all_gather(scaled, 'tensor', axis=0, tiled=True)]
    all_gather x1, waiting for transfers between devices: 74.7 us -> 1.01 us  [body(): whole_columns = lax.all_gather(column_basis, 'tensor', axis=1, tiled=True)]
    ppermute x0 -> x3, starting transfers between devices: none -> 32.7 us  [supply_the_point(): views.append(lax.ppermute(views[-1], net_axis, trail))]
    psum x1, waiting for transfers between devices: 27.3 us -> 1.31 us  [body(): core_mat = lax.psum(core_part.astype(jnp.bfloat16), 'tensor')]
  transfers between devices with their start and end apart: 4 -> 6, of which waited for: 4 -> 6; matrix products, arithmetic and copies ran while one was open for 4% -> 6% of each run, Pallas kernels for 0% -> 0%
where the time goes in v1:
time: 522 us; the launch traced here: 521 us
  waiting for transfers between devices  175 us (34%)
  blocking collectives  119 us (23%)
  local copies, waits for them, and re-layouts  89.7 us (17%)
  other arithmetic  57.8 us (11%)
  starting transfers between devices  32.8 us (6%)
  matrix products  30.3 us (6%)
  between operations  16 us (3%)
    ppermute x3, waiting for transfers between devices, supply_the_point(): views.append(lax.ppermute(views[-1], net_axis, trail))  96.5 us
    reduce_scatter x1, waiting for transfers between devices, body(): lax.psum_scatter(jnp.einsum('lrk,lrd->dlk', row_basis, group_block, prefe...  75.4 us
    all_to_all x1, blocking collectives, body(): lax.all_to_all(gradient, 'layer', split_axis=0, concat_axis=2, tiled=True)  54.5 us
    all_to_all x1, blocking collectives, body(): lax.all_to_all(rows_block, 'layer', split_axis=2, concat_axis=0, tiled=True)  53.6 us
    convert_element_type x1, local copies, waits for them, and re-layouts, finish(): return (raw_update * factor[:, None, None]).astype(jnp.bfloat16)  49.5 us
    unnamed x1, other arithmetic  43.5 us
    ppermute x3, starting transfers between devices, supply_the_point(): views.append(lax.ppermute(views[-1], net_axis, trail))  32.7 us
    unnamed x16, local copies, waits for them, and re-layouts  22.3 us
  transfers between devices with their start and end apart: 6, of which 6 were waited for; matrix products, arithmetic and copies ran while one was open for 6% of the time, Pallas kernels for 0%

profile of v1, /device:TPU:0, one launch (start us, length us, event | category | flops | bytes accessed | tf_op | source)
XLA Modules:
  0.0 520.7 jit_solution(6145690399948642083)
XLA Ops:
  6.5 0.0 copy-start
  6.5 0.0 reduce-scatter.2.cloned.1.call-start
  6.5 54.5 %all_to_all.36 = bf16[8,256,1024]{2,1,0:T(8,128)(2,1)} all-to-all(bf16[8,256,1024]{2,1,0:T(8,128)(2,1)} %param.7), channel_id=1, replica_groups=mesh['layer'=8,'tensor'=4] {'layer'}, dimensions={0} | all-to-all | bytes 8388608 | tf_op jit(solution)/shard_map/all_to_all | solution.py:52
  61.0 6.4 %copy.15 = bf16[1,256,8,1024]{1,3,2,0:T(8,128)(2,1)} copy(bf16[1,256,8,1024]{3,1,2,0:T(8,128)(2,1)} %bitcast.88) | data formatting | bytes 8388608 | tf_op jit(solution)/shard_map/all_to_all | solution.py:52
  67.4 0.0 copy-done
  67.4 5.4 %fusion.2 = bf16[8192,1,256]{2,0,1:T(8,128)(2,1)} fusion(bf16[256,8192]{0,1:T(8,128)(2,1)} %bitcast.85, bf16[1,256,256]{2,1,0:T(8,128)(2,1)S(1)} %copy-done), kind=kOutput, calls=%fused_computation.6 | convolution fusion | flops 1075838976 | bytes 8519680 | tf_op jit(solution)/shard_map/lrk,lrd->dlk/dot_general | solution.py:55
  72.8 0.0 copy-start.4
  72.8 0.0 copy-start.5
  72.8 0.0 reduce-scatter.2.cloned.1.call-update
  72.9 0.0 all-gather.2.cloned.1.call-start
  72.9 0.7 all-gather.2.cloned.1.call-update
  73.6 0.0 all-reduce.3.cloned.1.call-start
  74.4 0.0 copy-done.4
  74.4 75.4 %reduce-scatter.2.cloned.1.call-done = bf16[2048,1,256]{2,0,1:T(8,128)(2,1)} async-done(((bf16[8192,1,256]{2,0,1:T(8,128)(2,1)}), bf16[2048,1,256]{2,0,1:T(8,128)(2,1)}) %reduce-scatter.2.cloned.1.call-update) | async-done | bytes 1048592 | tf_op jit(solution)/shard_map/reduce_scatter | solution.py:54
  149.8 1.4 multiply_convert_fusion.1
  151.3 1.6 collective-permute-start
  152.8 39.4 %collective-permute-done = bf16[2048,1,256]{2,0,1:T(8,128)(2,1)} collective-permute-done((bf16[2048,1,256]{2,0,1:T(8,128)(2,1)S(1)}, bf16[2048,1,256]{2,0,1:T(8,128)(2,1)}, u32[]{:S(2)}, u32[]{:S(2)}) %collective-permute-start) | collective-permute-done | bytes 1048608 | tf_op jit(solution)/shard_map/ppermute | solution.py:22
  192.3 18.1 %collective-permute-start.1 = (bf16[2048,1,256]{2,0,1:T(8,128)(2,1)}, bf16[2048,1,256]{2,0,1:T(8,128)(2,1)}, u32[]{:S(2)}, u32[]{:S(2)}) collective-permute-start(bf16[2048,1,256]{2,0,1:T(8,128)(2,1)} %collective-permute-done), channel_id=1, source_target_pairs={{0,1},{1,2},{2,3},{3,0},{4,5},{5,6},{6,7},{7,4},{8,9},{9,10},{10,1... | collective-permute-start | bytes 3145736 | tf_op jit(solution)/shard_map/ppermute | solution.py:22
  211.1 0.0 copy-done.5
  211.1 5.0 multiply_reduce_fusion.1
  216.1 0.0 copy-start.2
  216.1 0.0 copy-start.3
  216.1 38.0 %collective-permute-done.1 = bf16[2048,1,256]{2,0,1:T(8,128)(2,1)} collective-permute-done((bf16[2048,1,256]{2,0,1:T(8,128)(2,1)}, bf16[2048,1,256]{2,0,1:T(8,128)(2,1)}, u32[]{:S(2)}, u32[]{:S(2)}) %collective-permute-start.1) | collective-permute-done | bytes 1048608 | tf_op jit(solution)/shard_map/ppermute | solution.py:22
  254.1 13.1 %collective-permute-start.2 = (bf16[2048,1,256]{2,0,1:T(8,128)(2,1)}, bf16[2048,1,256]{2,0,1:T(8,128)(2,1)}, u32[]{:S(2)}, u32[]{:S(2)}) collective-permute-start(bf16[2048,1,256]{2,0,1:T(8,128)(2,1)} %collective-permute-done.1), channel_id=1, source_target_pairs={{0,1},{1,2},{2,3},{3,0},{4,5},{5,6},{6,7},{7,4},{8,9},{9,10},{10,1... | collective-permute-start | bytes 3145736 | tf_op jit(solution)/shard_map/ppermute | solution.py:22
  267.2 1.0 all-gather.2.cloned.1.call-done
  268.2 4.7 fusion.9
  272.9 0.0 copy-done.2
  272.9 1.1 convolution_convert_fusion.1
  274.1 0.0 all-reduce.3.cloned.1.call-update
  274.1 0.0 copy-done.3
  274.1 0.2 fusion.28
  274.3 19.0 %collective-permute-done.2 = bf16[2048,1,256]{2,0,1:T(8,128)(2,1)} collective-permute-done((bf16[2048,1,256]{2,0,1:T(8,128)(2,1)}, bf16[2048,1,256]{2,0,1:T(8,128)(2,1)}, u32[]{:S(2)}, u32[]{:S(2)}) %collective-permute-start.2) | collective-permute-done | bytes 1048608 | tf_op jit(solution)/shard_map/ppermute | solution.py:22
  293.3 3.6 maximum_bitcast_fusion
  296.9 5.0 gather_fusion
  301.9 8.0 %fusion.1 = f32[256,8192]{0,1:T(8,128)} fusion(bf16[8192,256]{1,0:T(8,128)(2,1)} %bitcast.91, bf16[256,8192]{0,1:T(8,128)(2,1)} %bitcast.87, f32[]{:T(128)} %bitcast.4, f32[]{:T(128)} %bitcast, bf16[1,256,256]{2,1,0:T(8,128)(2,1)S(1)} %copy-done), kind=kOutput, calls=%fused_computation.4 | convolution fusion | flops 1082130432 | bytes 16908296 | tf_op jit(solution)/shard_map/lrk,dlk->lrd/dot_general | solution.py:69
  309.9 1.3 all-reduce.3.cloned.1.call-done
  311.2 11.0 %multiply_reduce_fusion = (f32[]{:T(128)}, f32[256,8192]{0,1:T(8,128)}) fusion(f32[256,8192]{0,1:T(8,128)} %fusion.1, bf16[1,8192,256]{2,1,0:T(8,128)(2,1)} %all-gather.2.cloned.1.call-done, f32[256,256]{1,0:T(8,128)S(1)} %fusion.9, bf16[256,256]{1,0:T(8,128)(2,1)} %all-reduce.3.cloned.1.call-done, bf16[1,256,256]{2,1,0:T(8,128)(2,1)S(1)} %copy-done, ...), kind=kOutput, calls=%fused_computation.8 | convolution fusion | flops 1113784320 | bytes 21496836 | tf_op jit(solution)/shard_map/lrk,ldk->lrd/dot_general | solution.py:80
  322.2 11.3 %all-reduce = (f32[1]{0:T(128)}, f32[1]{0:T(128)}) all-reduce(f32[1]{0:T(128)} %bitcast.25, f32[1]{0:T(128)} %bitcast.26), channel_id=1, replica_groups=mesh['layer'=8,'tensor'=4] {'tensor'}, use_global_device_ids=true, to_apply=%region_3.0 | all-reduce | flops 2 | bytes 16 | tf_op jit(solution)/shard_map/psum | solution.py:38
  334.8 4.1 fusion.3
  338.8 49.5 %copy.24 = bf16[1,256,8192]{1,0,2:T(2,128)(2,1)} copy(bf16[1,256,8192]{1,2,0:T(8,128)(2,1)S(1)} %fusion.3) | data formatting | bytes 8388608 | tf_op jit(solution)/shard_map/convert_element_type | solution.py:44
  388.4 0.5 broadcast.92
  388.9 43.5 %reduce.4 = bf16[8192,256]{1,0:T(8,128)(2,1)} reduce(bf16[8192,1,256]{2,1,0:T(2,128)(2,1)} %bitcast.89, bf16[]{:T(256)} %broadcast.92), dimensions={1}, to_apply=%bitcast.82.reduce_sub_computation | reduce | bytes 8388610
  432.4 7.0 %reshape.152 = bf16[8,2,131072]{2,1,0:T(2,128)(2,1)} reshape(bf16[8192,256]{1,0:T(8,128)(2,1)} %reduce.4) | data formatting | bytes 8388608
  439.4 53.6 %all_to_all.37 = bf16[8,2,131072]{2,1,0:T(2,128)(2,1)} all-to-all(bf16[8,2,131072]{2,1,0:T(2,128)(2,1)} %reshape.152), channel_id=1, replica_groups=mesh['layer'=8,'tensor'=4] {'layer'}, dimensions={0} | all-to-all | bytes 8388608 | tf_op jit(solution)/shard_map/all_to_all | solution.py:84
  492.9 8.7 %reshape.153 = bf16[8192,1,256]{2,1,0:T(2,128)(2,1)} reshape(bf16[8,2,131072]{2,1,0:T(2,128)(2,1)} %all_to_all.37) | data formatting | bytes 8388608
  501.7 6.1 %copy.22 = bf16[1,256,8192]{1,2,0:T(8,128)(2,1)} copy(bf16[1,256,8192]{1,0,2:T(2,128)(2,1)} %bitcast.90) | data formatting | bytes 8388608
  507.7 6.5 %copy.19 = bf16[8,256,1024]{2,1,0:T(8,128)(2,1)} copy(bf16[8,256,1024]{1,2,0:T(8,128)(2,1)} %bitcast.92) | data formatting | bytes 8388608 | tf_op jit(solution)/shard_map/all_to_all | solution.py:84
  514.2 0.0 copy-done.1
  (5 shorter events, 0.0 us)
Async XLA Ops:
  6.5 60.9 %copy-start = (bf16[1,256,256]{2,1,0:T(8,128)(2,1)S(1)}, bf16[1,256,256]{2,1,0:T(8,128)(2,1)}, u32[]{:S(2)}) copy-start(bf16[1,256,256]{2,1,0:T(8,128)(2,1)} %param.8) | copy-start | bytes 393220
  6.5 143.3 %reduce-scatter.2.cloned.1.call-start = ((), (), s32[]{:S(2)}) async-start(), calls=%async_computation.3 | async-start | bytes 5242880 | tf_op jit(solution)/shard_map/reduce_scatter | solution.py:54
  72.8 1.5 copy-start.4
  72.8 138.2 %copy-start.5 = (f32[1,256]{1,0:T(1,128)S(1)}, f32[1,256]{1,0:T(1,128)}, u32[]{:S(2)}) copy-start(f32[1,256]{1,0:T(1,128)} %param.11) | copy-start | bytes 3076
  72.9 195.3 %all-gather.2.cloned.1.call-start = ((), (), s32[]{:S(2)}) async-start(), calls=%async_computation.4 | async-start | bytes 5242880 | tf_op jit(solution)/shard_map/all_gather | solution.py:65
  73.6 237.6 %all-reduce.3.cloned.1.call-start = ((), (), s32[]{:S(2)}) async-start(), calls=%async_computation.5 | async-start | bytes 262144 | tf_op jit(solution)/shard_map/psum | solution.py:64
  151.3 41.0 %collective-permute-start = (bf16[2048,1,256]{2,0,1:T(8,128)(2,1)S(1)}, bf16[2048,1,256]{2,0,1:T(8,128)(2,1)}, u32[]{:S(2)}, u32[]{:S(2)}) collective-permute-start(bf16[2048,1,256]{2,0,1:T(8,128)(2,1)S(1)} %multiply_convert_fusion.1), channel_id=1, source_target_pairs={{0,1},{1,2},{2,3},{3,0},{4,5},{5,6},{6,7},{7,4},{8,9},{9,10},{10,1... | collective-permute-start | bytes 3145736 | tf_op jit(solution)/shard_map/ppermute | solution.py:22
  192.3 61.8 %collective-permute-start.1 = (bf16[2048,1,256]{2,0,1:T(8,128)(2,1)}, bf16[2048,1,256]{2,0,1:T(8,128)(2,1)}, u32[]{:S(2)}, u32[]{:S(2)}) collective-permute-start(bf16[2048,1,256]{2,0,1:T(8,128)(2,1)} %collective-permute-done), channel_id=1, source_target_pairs={{0,1},{1,2},{2,3},{3,0},{4,5},{5,6},{6,7},{7,4},{8,9},{9,10},{10,1... | collective-permute-start | bytes 3145736 | tf_op jit(solution)/shard_map/ppermute | solution.py:22
  216.1 56.9 %copy-start.2 = (bf16[1,2048,256]{2,1,0:T(8,128)(2,1)S(1)}, bf16[1,2048,256]{2,1,0:T(8,128)(2,1)}, u32[]{:S(2)}) copy-start(bf16[1,2048,256]{2,1,0:T(8,128)(2,1)} %param.9) | copy-start | bytes 3145732
  216.1 58.0 %copy-start.3 = (bf16[2048,1,256]{2,0,1:T(8,128)(2,1)S(1)}, bf16[2048,1,256]{2,0,1:T(8,128)(2,1)}, u32[]{:S(2)}) copy-start(bf16[2048,1,256]{2,0,1:T(8,128)(2,1)} %reduce-scatter.2.cloned.1.call-done) | copy-start | bytes 3145732
  254.1 39.2 %collective-permute-start.2 = (bf16[2048,1,256]{2,0,1:T(8,128)(2,1)}, bf16[2048,1,256]{2,0,1:T(8,128)(2,1)}, u32[]{:S(2)}, u32[]{:S(2)}) collective-permute-start(bf16[2048,1,256]{2,0,1:T(8,128)(2,1)} %collective-permute-done.1), channel_id=1, source_target_pairs={{0,1},{1,2},{2,3},{3,0},{4,5},{5,6},{6,7},{7,4},{8,9},{9,10},{10,1... | collective-permute-start | bytes 3145736 | tf_op jit(solution)/shard_map/ppermute | solution.py:22
  507.7 6.5 %copy-start.1 = (bf16[1,256,256]{2,1,0:T(8,128)(2,1)S(1)}, bf16[1,256,256]{2,1,0:T(8,128)(2,1)}, u32[]{:S(2)}) copy-start(bf16[1,256,256]{2,1,0:T(8,128)(2,1)} %param.8) | copy-start | bytes 393220
Sparse Core Ops, SparseCore 0:
  73.0 76.7 reduce-scatter.1
  151.4 116.7 all-gather.1
  274.2 36.9 all-reduce.2
